TPU v7x, 128 devices: a whole 4x4x4 slice. The times are simulated.
128 devices in a mesh: batch: 1, outer: 2 (over core), rows: 64 (over z, y, x).
Axes of the slice: x: 4, y: 4, z: 4, core: 2. Of those that a mesh axis runs over, the one named last changes fastest.
Arguments:
- a_mat: float32 [131072, 768], P(('batch', 'outer', 'rows'))
Outputs:
- output 1: float32 [131072, 768], P(('batch', 'outer', 'rows'))
- output 2: float32 [768, 768], P('batch')
All inputs are finite; a program needn't handle non-finite values.
Results may differ from a plain program's by a relative error of at most 0.001.
Values sent between devices are 32-bit elements.
A program may use at most 1 GiB of HBM per device.

v0:
```python
import jax
import jax.numpy as jnp
from jax import lax
from jax.experimental import pallas as pl
from jax.experimental.pallas import tpu as pltpu
from jax.sharding import PartitionSpec as P

MESH = pl.DeviceIdType.MESH
HI = lax.Precision.HIGHEST
NT = ((1,), (1,))
N = 768
NB = 6
NCH = 64
CHUNKS = ((0, 2, 0), (2, 4, 24), (4, 5, 16), (5, 6, 56))
BLKS = tuple(tuple((i, j) for i in range(a, b) for j in range(i + 1)) for a, b, _ in CHUNKS)
UNITS = tuple(8 * len(b) for b in BLKS)


def dot(a, b, dims):
    return lax.dot_general(a, b, (dims, ((), ())), precision=HI, preferred_element_type=jnp.float32)


def m8(v):
    return pl.multiple_of(v, 8)


def rb(i, j=None):
    return slice(128 * i, 128 * (i + 1 if j is None else j))


def bl(x, l):
    return jnp.broadcast_to(x[:, l:l + 1], (8, 128))

def bs(x, s):
    return jnp.broadcast_to(x[s:s + 1, :], (8, 128))

def factor(dref, uref, mref):
    sub = lax.broadcasted_iota(jnp.int32, (8, 128), 0)
    lane = lax.broadcasted_iota(jnp.int32, (8, 128), 1)
    zero = jnp.zeros((8, 128), jnp.float32)
    A = [dref[8 * i:8 * i + 8, :] for i in range(16)]
    for sp in range(8):
        l0 = 16 * sp
        ia, ib = 2 * sp, 2 * sp + 1
        blk = (lane >= l0) & (lane < l0 + 16)
        Ua, Ub = A[ia], A[ib]
        ca = [bl(Ua, l0 + s) for s in range(8)]
        cb = [bl(Ub, l0 + s) for s in range(16)]
        urg = [n for n in (ia + 2, ia + 3) if n < 16]
        cn = {n: [bl(A[n], l0 + s) for s in range(16)] for n in urg}
        Wa = jnp.where(blk, jnp.where(lane == sub + l0, 1.0, zero), Ua)
        Wb = jnp.where(blk, jnp.where(lane == sub + (l0 + 8), 1.0, zero), Ub)
        for n in range(ia + 2, 16):
            A[n] = jnp.where(blk, zero, A[n])
        for s in range(16):
            first = s < 8
            r = s % 8
            ri = lax.rsqrt(bs(ca[s] if first else cb[s], r))
            lb = cb[s] * ri
            if first:
                la = ca[s] * ri
                L = {t: (bs(la, t) if t < 8 else bs(lb, t - 8)) for t in range(s + 1, 16)}
                for t in range(s + 1, 8):
                    ca[t] = ca[t] - la * L[t]
                ma = jnp.where(sub > r, la, zero)
                u, w = bs(Ua, r) * ri, bs(Wa, r) * ri
                Ua = jnp.where(sub == r, u, Ua - ma * u)
                Wa = jnp.where(sub == r, w, Wa - ma * w)
                Ub = Ub - lb * u
                Wb = Wb - lb * w
            else:
                L = {t: bs(lb, t - 8) for t in range(s + 1, 16)}
                mb = jnp.where(sub > r, lb, zero)
                u, w = bs(Ub, r) * ri, bs(Wb, r) * ri
                Ub = jnp.where(sub == r, u, Ub - mb * u)
                Wb = jnp.where(sub == r, w, Wb - mb * w)
            for t in range(s + 1, 16):
                cb[t] = cb[t] - lb * L[t]
            for n in urg:
                ln = cn[n][s] * ri
                for t in range(s + 1, 16):
                    cn[n][t] = cn[n][t] - ln * L[t]
                A[n] = A[n] - ln * w
        uref[l0:l0 + 8, :] = jnp.where(lane >= sub + l0, Ua, zero)
        uref[l0 + 8:l0 + 16, :] = jnp.where(lane >= sub + (l0 + 8), Ub, zero)
        keep = lane < l0 + 16
        mref[l0:l0 + 8, :] = jnp.where(keep, Wa, zero)
        mref[l0 + 8:l0 + 16, :] = jnp.where(keep, Wb, zero)
        if ia + 4 < 16:
            W = jnp.concatenate([Wa, Wb], axis=0)
            D = dot(W, W, ((0,), (0,)))
            for n in range(ia + 4, 16):
                A[n] = A[n] - D[8 * n:8 * n + 8, :]


class Sum:
    def __init__(self, ch, c, me, bufs, sems):
        self.ch, self.c, self.me, self.other = ch, c, me, 1 - c
        self.p, self.recv0, self.acc, self.recv1, self.o, self.red = bufs
        self.s0, self.r0, self.s1, self.r1, self.s2, self.r2, self.s3, self.r3 = sems
        self.U = UNITS[ch]
        self.half = 8 * self.U
        self.base = CHUNKS[ch][2]
        self.mine = pl.ds(m8(c * self.half), self.half)
        self.unit = lax.rem(me - self.base + NCH, NCH)

    def gram(self, x):
        a, b, _ = CHUNKS[self.ch]
        full = dot(x[:, rb(a, b)], x[:, rb(0, b)], ((0,), (0,)))
        for n, (i, j) in enumerate(BLKS[self.ch]):
            self.p[rb(n), :] = full[rb(i - a), rb(j)]

    def exch(self, ref, dst, s, r, sl):
        return pltpu.make_async_remote_copy(ref.at[sl], dst, s, r, device_id=(0, self.other, self.me), device_id_type=MESH)

    def swap(self):
        sl = pl.ds(m8(self.other * self.half), self.half)
        self.cp0 = self.exch(self.p, self.recv0, self.s0, self.r0, sl)
        self.cp0.start()

    def scatter(self):
        self.exch(self.p, self.recv0, self.s0, self.r0, self.mine).wait_recv()
        self.acc[...] = self.p[self.mine] + self.recv0[...]

        def send(i, _):
            u = lax.rem(self.me + i, self.U)
            peer = lax.rem(self.base + u, NCH)
            k = lax.rem(peer - self.me + NCH, NCH)

            @pl.when(k > 0)
            def _():
                pltpu.make_async_remote_copy(self.acc.at[pl.ds(m8(8 * u), 8)], self.recv1.at[pl.ds(m8(8 * k - 8), 8)], self.s1, self.r1, device_id=(0, self.c, peer), device_id_type=MESH).start()
            return 0
        lax.fori_loop(0, self.U, send, 0)

    def rows(self, n, s, r):
        return pltpu.make_async_remote_copy(self.recv1.at[pl.ds(0, 8 * n)], self.recv1.at[pl.ds(0, 8 * n)], s, r, device_id=(0, self.other, self.me), device_id_type=MESH)

    def reduce(self):
        @pl.when(self.unit < self.U)
        def _():
            self.rows(63, self.s1, self.r1).wait_recv()
            t = [self.acc[pl.ds(m8(8 * self.unit), 8)]] + [self.recv1[8 * k:8 * k + 8, :] for k in range(63)]
            while len(t) > 1:
                t = [t[i] + t[i + 1] for i in range(0, len(t), 2)]
            self.red[...] = t[0]
            dst = pl.ds(m8(self.c * self.half + 8 * self.unit), 8)

            def send(k, _):
                peer = lax.rem(self.me + k, NCH)
                pltpu.make_async_remote_copy(self.red, self.o.at[dst], self.s2, self.r2, device_id=(0, self.c, peer), device_id_type=MESH).start()
                return 0
            lax.fori_loop(1, NCH, send, 0)
            self.o[dst] = t[0]

    def gather(self):
        @pl.when(self.unit < self.U)
        def _():
            self.rows(self.U - 1, self.s2, self.r2).wait_recv()

        @pl.when(self.unit >= self.U)
        def _():
            self.rows(self.U, self.s2, self.r2).wait_recv()
        self.exch(self.o, self.o.at[self.mine], self.s3, self.r3, self.mine).start()

    def finish(self, g):
        self.exch(self.o, self.o.at[self.mine], self.s3, self.r3, self.mine).wait_recv()
        for n, (i, j) in enumerate(BLKS[self.ch]):
            g[rb(i), rb(j)] = self.o[rb(n), :]

    def drain(self):
        self.exch(self.p, self.recv0, self.s0, self.r0, self.mine).wait_send()
        self.exch(self.o, self.o.at[self.mine], self.s3, self.r3, self.mine).wait_send()

        @pl.when(self.unit < self.U)
        def _():
            self.rows(self.U - 1, self.s1, self.r1).wait_send()
            self.rows(63, self.s2, self.r2).wait_send()

        @pl.when(self.unit >= self.U)
        def _():
            self.rows(self.U, self.s1, self.r1).wait_send()


def greet(c, me):
    bar = pltpu.get_barrier_semaphore()
    pl.semaphore_signal(bar, inc=1, device_id=(0, 1 - c, me), device_id_type=MESH)

    def sig(k, _):
        pl.semaphore_signal(bar, inc=1, device_id=(0, c, lax.rem(me + k, NCH)), device_id_type=MESH)
        return 0
    lax.fori_loop(1, NCH, sig, 0)
    return bar


def eliminate(j, a, b, g, l, w):
    if a < b:
        v = dot(g[rb(a, b), rb(j)], w[rb(j), wl(j)], NT)
        l[rb(a, b), rb(j)] = v
        for m in range(j + 1, b, 2):
            lo, hi = max(a, m), min(m + 2, b)
            g[rb(lo, b), rb(m, hi)] = g[rb(lo, b), rb(m, hi)] - dot(v[128 * (lo - a):, :], l[rb(m, hi), rb(j)], NT)


def wl(k):
    return rb(k % 2)


def pair(k, l, w):
    w[rb(k), rb(0)] = -dot(w[rb(k), rb(1)], dot(l[rb(k), rb(k - 1)], w[rb(k - 1), rb(0)], ((1,), (0,))), ((1,), (0,)))


def solve_cols(x_ref, l, w, q_ref, a, b, step=256):
    def rows(r, _):
        sl = pl.ds(pl.multiple_of(step * r, step), step)
        t = x_ref[sl, rb(a, b)]
        if a:
            t = t - dot(q_ref[sl, rb(0, a)], l[rb(a, b), rb(0, a)], NT)
        q_ref[sl, rb(a, b)] = dot(t, w[rb(a, b), :] if b - a == 2 else w[rb(a), wl(a)], NT)
        return 0
    lax.fori_loop(0, x_ref.shape[0] // step, rows, 0)


JOIN = ((-1, 1, 2, 2), (5, 7, 8, 10))
GATHER = ((-1, 0, 1, 1), (4, 6, 7, 9))
REDUCE = ((-1, -1, -1, 0), (3, 5, 6, 8))
SCATTER = ((-1, -1, -1, -1), (2, 4, 5, 6))
APPLY = {1: 0, 3: 1, 4: 2, 5: 3}


def main_kernel(x, q, w2, l1, l2, g, w1, dbuf, ubuf, mbuf, *rest):
    c, me = lax.axis_index("outer"), lax.axis_index("rows")
    bar = greet(c, me)
    nc = len(CHUNKS)
    bufs, sems = rest[:12 * nc], rest[12 * nc:]
    S = [[Sum(ch, c, me, bufs[6 * (nc * s + ch):6 * (nc * s + ch) + 6], [r.at[s, ch] for r in sems]) for ch in range(nc)] for s in range(2)]
    S0, S1 = S
    for r in (w1, w2, l1, l2):
        r[...] = jnp.zeros_like(r)
    S0[0].gram(x)
    S0[1].gram(x)
    pl.semaphore_wait(bar, NCH)
    S0[0].swap()
    S0[1].swap()
    S0[2].gram(x)
    S0[2].swap()
    S0[0].scatter()
    S0[1].scatter()
    S0[3].gram(x)
    S0[3].swap()
    S0[2].scatter()
    S0[0].reduce()
    S0[3].scatter()
    S0[1].reduce()
    S0[2].reduce()
    S0[0].gather()
    S0[0].finish(g)
    dbuf[...] = g[rb(0), rb(0)]

    def section(t):
        s, k = divmod(t, NB)
        l, w = ((l1, w1), (l2, w2))[s]
        for ss in range(2):
            for ch in range(nc):
                if SCATTER[ss][ch] == t:
                    S[ss][ch].scatter()
        for ss in range(2):
            for ch in range(nc):
                if REDUCE[ss][ch] == t:
                    S[ss][ch].reduce()
        for ss in range(2):
            for ch in range(nc):
                if GATHER[ss][ch] == t:
                    S[ss][ch].gather()
        w[rb(k), wl(k)] = mbuf[...]
        l[rb(k), rb(k)] = ubuf[...].T
        end = max(CHUNKS[ch][1] for ch in range(nc) if JOIN[s][ch] < t)
        eliminate(k, k + 1, end, g, l, w)
        for ch in range(nc):
            if JOIN[s][ch] == t:
                S[s][ch].finish(g)
                a, b, _ = CHUNKS[ch]
                for j in range(k + 1):
                    eliminate(j, a, b, g, l, w)
        if k < NB - 1:
            dbuf[...] = g[rb(k + 1), rb(k + 1)]
        if k % 2:
            pair(k, l, w)
        if t in APPLY:
            ch = APPLY[t]
            a, b, _ = CHUNKS[ch]
            solve_cols(x, l, w, q, a, b)
            S1[ch].gram(q)
            S1[ch].swap()
        if t == NB - 1:
            S1[0].finish(g)
            dbuf[...] = g[rb(0), rb(0)]

    def step(t, _):
        factor(dbuf, ubuf, mbuf)
        for tt in range(2 * NB):
            @pl.when(t == tt)
            def _():
                section(tt)
        return 0

    lax.fori_loop(0, 2 * NB, step, 0)
    for s in S:
        for ch in s:
            ch.drain()


def last_kernel(x, w, l2, l1, q, r):
    for j in range(3):
        solve_cols(x, l2, w, q, 2 * j, 2 * j + 2)
    for i in range(3):
        for j in range(i):
            r[rb(2 * i, 2 * i + 2), rb(2 * j, 2 * j + 2)] = jnp.zeros((256, 256), jnp.float32)

    def blk(i):
        return pl.ds(pl.multiple_of(256 * i, 256), 256)

    def diag(w):
        def f(i, _):
            k = pl.ds(pl.multiple_of(256 * i, 256), 256 * (w + 1))
            r[blk(i), blk(i + w)] = dot(l2[k, blk(i)], l1[blk(i + w), k], ((0,), (1,)))
            return 0
        lax.fori_loop(0, 3 - w, f, 0)
    for w in range(3):
        diag(w)


def solution(mesh):
    spec = P(("batch", "outer", "rows"), None)
    V = pl.BlockSpec(memory_space=pltpu.VMEM)
    F = lambda *s: jax.ShapeDtypeStruct(s, jnp.float32)
    B = lambda *s: pltpu.VMEM(s, jnp.float32)
    bufs = []
    for u in 2 * UNITS:
        bufs += [B(16 * u, 128), B(8 * u, 128), B(8 * u, 128), B(504, 128), B(16 * u, 128), B(8, 128)]

    def local_qr(a):
        q1, w2, l1, l2 = pl.pallas_call(
            main_kernel, out_shape=(F(*a.shape), F(N, 256), F(N, N), F(N, N)), in_specs=[V], out_specs=(V,) * 4,
            scratch_shapes=[B(N, N), B(N, 256), B(128, 128), B(128, 128), B(128, 128)] + bufs + [pltpu.SemaphoreType.DMA((2, len(CHUNKS)))] * 8,
            compiler_params=pltpu.CompilerParams(vmem_limit_bytes=34 * 2**20, collective_id=0, has_side_effects=True), name="sweeps")(a)
        return tuple(pl.pallas_call(
            last_kernel, out_shape=(F(*a.shape), F(N, N)), in_specs=[V] * 4, out_specs=(V, V),
            compiler_params=pltpu.CompilerParams(vmem_limit_bytes=20 * 2**20), name="last")(q1, w2, l2, l1))

    return jax.shard_map(local_qr, mesh=mesh, in_specs=(spec,), out_specs=(spec, P("batch", None)), check_vma=False)
```

profile of v0, /device:TPU:1, one launch (start us, length us, event | category | flops | bytes accessed | tf_op | source)
XLA Modules:
  0.0 136.6 jit_solution(11303964826762807634)
XLA Ops:
  0.6 0.0 copy-start
  0.6 1.9 %copy-done = f32[1024,768]{1,0:T(8,128)S(1)} copy-done((f32[1024,768]{1,0:T(8,128)S(1)}, f32[1024,768]{1,0:T(8,128)}, u32[]{:S(2)}) %copy-start) | copy-done | bytes 3145752
  2.5 117.7 %sweeps.1 = (f32[1024,768]{1,0:T(8,128)S(1)}, f32[768,256]{1,0:T(8,128)S(1)}, f32[768,768]{1,0:T(8,128)S(1)}, f32[768,768]{1,0:T(8,128)S(1)}) custom-call(f32[1024,768]{1,0:T(8,128)S(1)} %copy-done), custom_call_target="tpu_custom_call" | custom-call | tf_op jit(solution)/shard_map/sweeps/pallas_call | solution.py:343
  120.3 16.4 %last.1 = (f32[1024,768]{1,0:T(8,128)}, f32[768,768]{1,0:T(8,128)}) custom-call(f32[1024,768]{1,0:T(8,128)S(1)} %get-tuple-element.6.x, f32[768,256]{1,0:T(8,128)S(1)} %get-tuple-element.7.w, f32[768,768]{1,0:T(8,128)S(1)} %get-tuple-element.8.l2, f32[768,768]{1,0:T(8,128)S(1)} %get-tuple-element.9.l1), custom_call_target="tpu_custom_call" | custom-call | tf_op jit(solution)/shard_map/last/pallas_call | solution.py:347
Async XLA Ops:
  0.6 1.9 %copy-start = (f32[1024,768]{1,0:T(8,128)S(1)}, f32[1024,768]{1,0:T(8,128)}, u32[]{:S(2)}) copy-start(f32[1024,768]{1,0:T(8,128)} %x.1) | copy-start | bytes 9437188
where the time goes:
time: 137 us
  Pallas kernels  134 us (98%)
  local copies, waits for them, and re-layouts  1.88 us (1%)
    pallas_call x1, Pallas kernels, local_qr(): pl.pallas_call(main_kernel, out_shape=(F(*a.shape), F(N, 256), F(N, N), F...  118 us
    pallas_call x1, Pallas kernels, local_qr(): pl.pallas_call(last_kernel, out_shape=(F(*a.shape), F(N, N)), in_specs=[V...  16.4 us

commit v1 on v0

--- a/solution.py
+++ b/solution.py
@@ -11,9 +11,10 @@
 N = 768
 NB = 6
 NCH = 64
-CHUNKS = ((0, 2, 0), (2, 4, 24), (4, 5, 16), (5, 6, 56))
+CHUNKS = ((0, 2, 0), (2, 4, 12), (4, 5, 40), (5, 6, 60))
 BLKS = tuple(tuple((i, j) for i in range(a, b) for j in range(i + 1)) for a, b, _ in CHUNKS)
-UNITS = tuple(8 * len(b) for b in BLKS)
+UT = 16
+UNITS = tuple(64 * len(b) // UT for b in BLKS)
 
 
 def dot(a, b, dims):
@@ -22,6 +23,10 @@
 
 def m8(v):
     return pl.multiple_of(v, 8)
+
+
+def wrap(v):
+    return jnp.where(v >= NCH, v - NCH, v)
 
 
 def rb(i, j=None):
@@ -99,10 +104,10 @@
         self.p, self.recv0, self.acc, self.recv1, self.o, self.red = bufs
         self.s0, self.r0, self.s1, self.r1, self.s2, self.r2, self.s3, self.r3 = sems
         self.U = UNITS[ch]
-        self.half = 8 * self.U
-        self.base = CHUNKS[ch][2]
+        self.half = UT * self.U
+        self.base = wrap(CHUNKS[ch][2] + 32 * c)
         self.mine = pl.ds(m8(c * self.half), self.half)
-        self.unit = lax.rem(me - self.base + NCH, NCH)
+        self.unit = wrap(me - self.base + NCH)
 
     def gram(self, x):
         a, b, _ = CHUNKS[self.ch]
@@ -121,36 +126,38 @@
     def scatter(self):
         self.exch(self.p, self.recv0, self.s0, self.r0, self.mine).wait_recv()
         self.acc[...] = self.p[self.mine] + self.recv0[...]
+        slot = pl.ds(m8(UT * self.me), UT)
+        first = lax.rem(self.me, self.U)
 
         def send(i, _):
-            u = lax.rem(self.me + i, self.U)
-            peer = lax.rem(self.base + u, NCH)
-            k = lax.rem(peer - self.me + NCH, NCH)
-
-            @pl.when(k > 0)
+            u = first + i
+            u = jnp.where(u >= self.U, u - self.U, u)
+            peer = wrap(self.base + u)
+
+            @pl.when(peer != self.me)
             def _():
-                pltpu.make_async_remote_copy(self.acc.at[pl.ds(m8(8 * u), 8)], self.recv1.at[pl.ds(m8(8 * k - 8), 8)], self.s1, self.r1, device_id=(0, self.c, peer), device_id_type=MESH).start()
+                pltpu.make_async_remote_copy(self.acc.at[pl.ds(m8(UT * u), UT)], self.recv1.at[slot], self.s1, self.r1, device_id=(0, self.c, peer), device_id_type=MESH).start()
             return 0
-        lax.fori_loop(0, self.U, send, 0)
+        lax.fori_loop(0, self.U, send, 0, unroll=4)
 
     def rows(self, n, s, r):
-        return pltpu.make_async_remote_copy(self.recv1.at[pl.ds(0, 8 * n)], self.recv1.at[pl.ds(0, 8 * n)], s, r, device_id=(0, self.other, self.me), device_id_type=MESH)
+        return pltpu.make_async_remote_copy(self.recv1.at[pl.ds(0, UT * n)], self.recv1.at[pl.ds(0, UT * n)], s, r, device_id=(0, self.other, self.me), device_id_type=MESH)
 
     def reduce(self):
         @pl.when(self.unit < self.U)
         def _():
+            self.recv1[pl.ds(m8(UT * self.me), UT)] = self.acc[pl.ds(m8(UT * self.unit), UT)]
             self.rows(63, self.s1, self.r1).wait_recv()
-            t = [self.acc[pl.ds(m8(8 * self.unit), 8)]] + [self.recv1[8 * k:8 * k + 8, :] for k in range(63)]
+            t = [self.recv1[UT * k:UT * k + UT, :] for k in range(NCH)]
             while len(t) > 1:
                 t = [t[i] + t[i + 1] for i in range(0, len(t), 2)]
             self.red[...] = t[0]
-            dst = pl.ds(m8(self.c * self.half + 8 * self.unit), 8)
+            dst = pl.ds(m8(self.c * self.half + UT * self.unit), UT)
 
             def send(k, _):
-                peer = lax.rem(self.me + k, NCH)
-                pltpu.make_async_remote_copy(self.red, self.o.at[dst], self.s2, self.r2, device_id=(0, self.c, peer), device_id_type=MESH).start()
+                pltpu.make_async_remote_copy(self.red, self.o.at[dst], self.s2, self.r2, device_id=(0, self.c, wrap(self.me + k)), device_id_type=MESH).start()
                 return 0
-            lax.fori_loop(1, NCH, send, 0)
+            lax.fori_loop(1, NCH, send, 0, unroll=7)
             self.o[dst] = t[0]
 
     def gather(self):
@@ -187,9 +194,9 @@
     pl.semaphore_signal(bar, inc=1, device_id=(0, 1 - c, me), device_id_type=MESH)
 
     def sig(k, _):
-        pl.semaphore_signal(bar, inc=1, device_id=(0, c, lax.rem(me + k, NCH)), device_id_type=MESH)
+        pl.semaphore_signal(bar, inc=1, device_id=(0, c, wrap(me + k)), device_id_type=MESH)
         return 0
-    lax.fori_loop(1, NCH, sig, 0)
+    lax.fori_loop(1, NCH, sig, 0, unroll=7)
     return bar
 
 
@@ -210,20 +217,23 @@
     w[rb(k), rb(0)] = -dot(w[rb(k), rb(1)], dot(l[rb(k), rb(k - 1)], w[rb(k - 1), rb(0)], ((1,), (0,))), ((1,), (0,)))
 
 
-def solve_cols(x_ref, l, w, q_ref, a, b, step=256):
+def solve_rows(x_ref, l, w, q_ref, a, b, sl):
+    t = x_ref[sl, rb(a, b)]
+    if a:
+        t = t - dot(q_ref[sl, rb(0, a)], l[rb(a, b), rb(0, a)], NT)
+    q_ref[sl, rb(a, b)] = dot(t, w[rb(a, b), :] if b - a == 2 else w[rb(a), wl(a)], NT)
+
+
+def solve_cols(x_ref, l, w, q_ref, a, b):
     def rows(r, _):
-        sl = pl.ds(pl.multiple_of(step * r, step), step)
-        t = x_ref[sl, rb(a, b)]
-        if a:
-            t = t - dot(q_ref[sl, rb(0, a)], l[rb(a, b), rb(0, a)], NT)
-        q_ref[sl, rb(a, b)] = dot(t, w[rb(a, b), :] if b - a == 2 else w[rb(a), wl(a)], NT)
+        solve_rows(x_ref, l, w, q_ref, a, b, pl.ds(pl.multiple_of(256 * r, 256), 256))
         return 0
-    lax.fori_loop(0, x_ref.shape[0] // step, rows, 0)
-
-
-JOIN = ((-1, 1, 2, 2), (5, 7, 8, 10))
-GATHER = ((-1, 0, 1, 1), (4, 6, 7, 9))
-REDUCE = ((-1, -1, -1, 0), (3, 5, 6, 8))
+    lax.fori_loop(0, x_ref.shape[0] // 256, rows, 0)
+
+
+JOIN = ((-1, 1, 2, 2), (5, 7, 9, 10))
+GATHER = ((-1, 0, 1, 1), (4, 7, 9, 10))
+REDUCE = ((-1, -1, -1, 0), (3, 5, 7, 8))
 SCATTER = ((-1, -1, -1, -1), (2, 4, 5, 6))
 APPLY = {1: 0, 3: 1, 4: 2, 5: 3}
 
@@ -237,22 +247,19 @@
     S0, S1 = S
     for r in (w1, w2, l1, l2):
         r[...] = jnp.zeros_like(r)
-    S0[0].gram(x)
-    S0[1].gram(x)
+    for ch in range(3):
+        S0[ch].gram(x)
     pl.semaphore_wait(bar, NCH)
-    S0[0].swap()
-    S0[1].swap()
-    S0[2].gram(x)
-    S0[2].swap()
-    S0[0].scatter()
-    S0[1].scatter()
+    for ch in range(3):
+        S0[ch].swap()
+    for ch in range(2):
+        S0[ch].scatter()
     S0[3].gram(x)
     S0[3].swap()
-    S0[2].scatter()
-    S0[0].reduce()
-    S0[3].scatter()
-    S0[1].reduce()
-    S0[2].reduce()
+    for ch in (2, 3):
+        S0[ch].scatter()
+    for ch in range(3):
+        S0[ch].reduce()
     S0[0].gather()
     S0[0].finish(g)
     dbuf[...] = g[rb(0), rb(0)]
@@ -310,34 +317,49 @@
             ch.drain()
 
 
-def last_kernel(x, w, l2, l1, q, r):
-    for j in range(3):
-        solve_cols(x, l2, w, q, 2 * j, 2 * j + 2)
+def last_kernel(x, w, l2, l1, qo, ro, q, r, sem):
+    def blk(i):
+        return pl.ds(pl.multiple_of(256 * i, 256), 256)
+
     for i in range(3):
         for j in range(i):
             r[rb(2 * i, 2 * i + 2), rb(2 * j, 2 * j + 2)] = jnp.zeros((256, 256), jnp.float32)
 
-    def blk(i):
-        return pl.ds(pl.multiple_of(256 * i, 256), 256)
-
-    def diag(w):
+    def diag(d):
         def f(i, _):
-            k = pl.ds(pl.multiple_of(256 * i, 256), 256 * (w + 1))
-            r[blk(i), blk(i + w)] = dot(l2[k, blk(i)], l1[blk(i + w), k], ((0,), (1,)))
+            k = pl.ds(pl.multiple_of(256 * i, 256), 256 * (d + 1))
+            r[blk(i), blk(i + d)] = dot(l2[k, blk(i)], l1[blk(i + d), k], ((0,), (1,)))
             return 0
-        lax.fori_loop(0, 3 - w, f, 0)
-    for w in range(3):
-        diag(w)
+        lax.fori_loop(0, 3 - d, f, 0)
+    for d in range(3):
+        diag(d)
+    out = pltpu.make_async_copy(r, ro, sem.at[0])
+    out.start()
+    half = x.shape[0] // 2
+
+    def rows(h, _):
+        sl = pl.ds(pl.multiple_of(half * h, half), half)
+        for j in range(3):
+            solve_rows(x, l2, w, q, 2 * j, 2 * j + 2, sl)
+        pltpu.make_async_copy(q.at[sl], qo.at[sl], sem.at[h + 1]).start()
+        return 0
+    lax.fori_loop(0, 2, rows, 0)
+    for h in range(2):
+        sl = pl.ds(half * h, half)
+        pltpu.make_async_copy(q.at[sl], qo.at[sl], sem.at[h + 1]).wait()
+    out.wait()
 
 
 def solution(mesh):
     spec = P(("batch", "outer", "rows"), None)
     V = pl.BlockSpec(memory_space=pltpu.VMEM)
+    H = pl.BlockSpec(memory_space=pl.ANY)
     F = lambda *s: jax.ShapeDtypeStruct(s, jnp.float32)
     B = lambda *s: pltpu.VMEM(s, jnp.float32)
     bufs = []
     for u in 2 * UNITS:
-        bufs += [B(16 * u, 128), B(8 * u, 128), B(8 * u, 128), B(504, 128), B(16 * u, 128), B(8, 128)]
+        h = UT * u
+        bufs += [B(2 * h, 128), B(h, 128), B(h, 128), B(UT * NCH, 128), B(2 * h, 128), B(UT, 128)]
 
     def local_qr(a):
         q1, w2, l1, l2 = pl.pallas_call(
@@ -345,7 +367,8 @@
             scratch_shapes=[B(N, N), B(N, 256), B(128, 128), B(128, 128), B(128, 128)] + bufs + [pltpu.SemaphoreType.DMA((2, len(CHUNKS)))] * 8,
             compiler_params=pltpu.CompilerParams(vmem_limit_bytes=34 * 2**20, collective_id=0, has_side_effects=True), name="sweeps")(a)
         return tuple(pl.pallas_call(
-            last_kernel, out_shape=(F(*a.shape), F(N, N)), in_specs=[V] * 4, out_specs=(V, V),
+            last_kernel, out_shape=(F(*a.shape), F(N, N)), in_specs=[V] * 4, out_specs=(H, H),
+            scratch_shapes=[B(*a.shape), B(N, N), pltpu.SemaphoreType.DMA((3,))],
             compiler_params=pltpu.CompilerParams(vmem_limit_bytes=20 * 2**20), name="last")(q1, w2, l2, l1))
 
     return jax.shard_map(local_qr, mesh=mesh, in_specs=(spec,), out_specs=(spec, P("batch", None)), check_vma=False)

time: 137 us -> 130 us (0.949)
  Pallas kernels: 134 us -> 127 us
    pallas_call x1, Pallas kernels: 118 us -> 113 us  [local_qr(): pl.pallas_call(main_kernel, out_shape=(F(*a.shape), F(N, 256), F(N, N), F...]
    pallas_call x1, Pallas kernels: 16.4 us -> 13.3 us  [local_qr(): pl.pallas_call(last_kernel, out_shape=(F(*a.shape), F(N, N)), in_specs=[V...]
where the time goes in v1:
time: 130 us; the launch traced here: 129 us
  Pallas kernels  127 us (98%)
  local copies, waits for them, and re-layouts  1.88 us (1%)
    pallas_call x1, Pallas kernels, local_qr(): pl.pallas_call(main_kernel, out_shape=(F(*a.shape), F(N, 256), F(N, N), F...  113 us
    pallas_call x1, Pallas kernels, local_qr(): pl.pallas_call(last_kernel, out_shape=(F(*a.shape), F(N, N)), in_specs=[V...  13.3 us

profile of v1, /device:TPU:1, one launch (start us, length us, event | category | flops | bytes accessed | tf_op | source)
XLA Modules:
  0.0 129.4 jit_solution(11112225592777590972)
XLA Ops:
  0.6 0.0 copy-start
  0.6 1.9 %copy-done = f32[1024,768]{1,0:T(8,128)S(1)} copy-done((f32[1024,768]{1,0:T(8,128)S(1)}, f32[1024,768]{1,0:T(8,128)}, u32[]{:S(2)}) %copy-start) | copy-done | bytes 3145752
  2.5 113.4 %sweeps.1 = (f32[1024,768]{1,0:T(8,128)S(1)}, f32[768,256]{1,0:T(8,128)S(1)}, f32[768,768]{1,0:T(8,128)S(1)}, f32[768,768]{1,0:T(8,128)S(1)}) custom-call(f32[1024,768]{1,0:T(8,128)S(1)} %copy-done), custom_call_target="tpu_custom_call" | custom-call | tf_op jit(solution)/shard_map/sweeps/pallas_call | solution.py:365
  116.0 13.3 %last.1 = (f32[1024,768]{1,0:T(8,128)}, f32[768,768]{1,0:T(8,128)}) custom-call(f32[1024,768]{1,0:T(8,128)S(1)} %get-tuple-element.6.x, f32[768,256]{1,0:T(8,128)S(1)} %get-tuple-element.7.w, f32[768,768]{1,0:T(8,128)S(1)} %get-tuple-element.8.l2, f32[768,768]{1,0:T(8,128)S(1)} %get-tuple-element.9.l1), custom_call_target="tpu_custom_call" | custom-call | tf_op jit(solution)/shard_map/last/pallas_call | solution.py:369
Async XLA Ops:
  0.6 1.9 %copy-start = (f32[1024,768]{1,0:T(8,128)S(1)}, f32[1024,768]{1,0:T(8,128)}, u32[]{:S(2)}) copy-start(f32[1024,768]{1,0:T(8,128)} %x.1) | copy-start | bytes 9437188

commit v2 on v1

--- a/solution.py
+++ b/solution.py
@@ -7,12 +7,14 @@
 
 MESH = pl.DeviceIdType.MESH
 HI = lax.Precision.HIGHEST
+NN = ((1,), (0,))
+TN = ((0,), (0,))
 NT = ((1,), (1,))
 N = 768
 NB = 6
 NCH = 64
 CHUNKS = ((0, 2, 0), (2, 4, 12), (4, 5, 40), (5, 6, 60))
-BLKS = tuple(tuple((i, j) for i in range(a, b) for j in range(i + 1)) for a, b, _ in CHUNKS)
+BLKS = tuple(tuple((i, j) for j in range(a, b) for i in range(j + 1)) for a, b, _ in CHUNKS)
 UT = 16
 UNITS = tuple(64 * len(b) // UT for b in BLKS)
 
@@ -107,13 +109,16 @@
         self.half = UT * self.U
         self.base = wrap(CHUNKS[ch][2] + 32 * c)
         self.mine = pl.ds(m8(c * self.half), self.half)
-        self.unit = wrap(me - self.base + NCH)
+        self.unit = lax.rem(13 * (me - self.base + NCH), NCH)
 
     def gram(self, x):
         a, b, _ = CHUNKS[self.ch]
-        full = dot(x[:, rb(a, b)], x[:, rb(0, b)], ((0,), (0,)))
+        if b - a == 2:
+            full = dot(x[:, rb(0, b)], x[:, rb(a, b)], TN)
+        else:
+            full = dot(x[:, rb(a, b)], x[:, rb(0, b)], TN)
         for n, (i, j) in enumerate(BLKS[self.ch]):
-            self.p[rb(n), :] = full[rb(i - a), rb(j)]
+            self.p[rb(n), :] = full[rb(i), rb(j - a)] if b - a == 2 else full[:, rb(i)].T
 
     def exch(self, ref, dst, s, r, sl):
         return pltpu.make_async_remote_copy(ref.at[sl], dst, s, r, device_id=(0, self.other, self.me), device_id_type=MESH)
@@ -132,7 +137,7 @@
         def send(i, _):
             u = first + i
             u = jnp.where(u >= self.U, u - self.U, u)
-            peer = wrap(self.base + u)
+            peer = lax.rem(self.base + 5 * u, NCH)
 
             @pl.when(peer != self.me)
             def _():
@@ -200,58 +205,64 @@
     return bar
 
 
-def eliminate(j, a, b, g, l, w):
+def eliminate(j, a, b, g, u, w):
     if a < b:
-        v = dot(g[rb(a, b), rb(j)], w[rb(j), wl(j)], NT)
-        l[rb(a, b), rb(j)] = v
+        v = dot(w[rb(j), :], g[rb(j), rb(a, b)], NN)
+        u[rb(j), rb(a, b)] = v
         for m in range(j + 1, b, 2):
             lo, hi = max(a, m), min(m + 2, b)
-            g[rb(lo, b), rb(m, hi)] = g[rb(lo, b), rb(m, hi)] - dot(v[128 * (lo - a):, :], l[rb(m, hi), rb(j)], NT)
-
-
-def wl(k):
-    return rb(k % 2)
-
-
-def pair(k, l, w):
-    w[rb(k), rb(0)] = -dot(w[rb(k), rb(1)], dot(l[rb(k), rb(k - 1)], w[rb(k - 1), rb(0)], ((1,), (0,))), ((1,), (0,)))
-
-
-def solve_rows(x_ref, l, w, q_ref, a, b, sl):
+            g[rb(m, hi), rb(lo, b)] = g[rb(m, hi), rb(lo, b)] - dot(u[rb(j), rb(m, hi)], v[:, 128 * (lo - a):], TN)
+
+
+def invert_pair(k, u, w, wt):
+    t = w[rb(k), :].T
+    wt[rb(k), rb(k % 2)] = t
+    if k % 2:
+        wt[rb(k - 1), rb(1)] = -dot(wt[rb(k - 1), rb(0)], dot(u[rb(k - 1), rb(k)], t, NN), NN)
+
+
+def solve_rows(x_ref, u, wt, q_ref, a, b, sl):
     t = x_ref[sl, rb(a, b)]
     if a:
-        t = t - dot(q_ref[sl, rb(0, a)], l[rb(a, b), rb(0, a)], NT)
-    q_ref[sl, rb(a, b)] = dot(t, w[rb(a, b), :] if b - a == 2 else w[rb(a), wl(a)], NT)
-
-
-def solve_cols(x_ref, l, w, q_ref, a, b):
+        t = t - dot(q_ref[sl, rb(0, a)], u[rb(0, a), rb(a, b)], NN)
+    q_ref[sl, rb(a, b)] = dot(t, wt[rb(a, b), :] if b - a == 2 else wt[rb(a), rb(a % 2)], NN)
+
+
+def solve_cols(x_ref, u, wt, q_ref, a, b):
     def rows(r, _):
-        solve_rows(x_ref, l, w, q_ref, a, b, pl.ds(pl.multiple_of(256 * r, 256), 256))
+        solve_rows(x_ref, u, wt, q_ref, a, b, pl.ds(pl.multiple_of(256 * r, 256), 256))
         return 0
     lax.fori_loop(0, x_ref.shape[0] // 256, rows, 0)
 
 
-JOIN = ((-1, 1, 2, 2), (5, 7, 9, 10))
-GATHER = ((-1, 0, 1, 1), (4, 7, 9, 10))
-REDUCE = ((-1, -1, -1, 0), (3, 5, 7, 8))
+JOIN = ((-1, 1, 2, 2), (5, 7, 8, 10))
+GATHER = ((-1, 0, 1, 1), (4, 6, 8, 10))
+REDUCE = ((-1, -1, -1, 0), (3, 5, 6, 8))
 SCATTER = ((-1, -1, -1, -1), (2, 4, 5, 6))
 APPLY = {1: 0, 3: 1, 4: 2, 5: 3}
 
 
-def main_kernel(x, q, w2, l1, l2, g, w1, dbuf, ubuf, mbuf, *rest):
+def main_kernel(xin, q, wt2, u1, u2, x, xsem, g, wt1, w, dbuf, ubuf, mbuf, *rest):
     c, me = lax.axis_index("outer"), lax.axis_index("rows")
+    load = [pltpu.make_async_copy(xin.at[:, rb(2 * j, 2 * j + 2)], x.at[:, rb(2 * j, 2 * j + 2)], xsem.at[j]) for j in range(3)]
+    for cp in load:
+        cp.start()
     bar = greet(c, me)
     nc = len(CHUNKS)
     bufs, sems = rest[:12 * nc], rest[12 * nc:]
     S = [[Sum(ch, c, me, bufs[6 * (nc * s + ch):6 * (nc * s + ch) + 6], [r.at[s, ch] for r in sems]) for ch in range(nc)] for s in range(2)]
     S0, S1 = S
-    for r in (w1, w2, l1, l2):
+    for r in (wt1, wt2, u1, u2):
         r[...] = jnp.zeros_like(r)
-    for ch in range(3):
+    for ch in range(2):
+        load[ch].wait()
         S0[ch].gram(x)
+    load[2].wait()
     pl.semaphore_wait(bar, NCH)
-    for ch in range(3):
+    for ch in range(2):
         S0[ch].swap()
+    S0[2].gram(x)
+    S0[2].swap()
     for ch in range(2):
         S0[ch].scatter()
     S0[3].gram(x)
@@ -266,7 +277,7 @@
 
     def section(t):
         s, k = divmod(t, NB)
-        l, w = ((l1, w1), (l2, w2))[s]
+        u, wt = ((u1, wt1), (u2, wt2))[s]
         for ss in range(2):
             for ch in range(nc):
                 if SCATTER[ss][ch] == t:
@@ -279,24 +290,23 @@
             for ch in range(nc):
                 if GATHER[ss][ch] == t:
                     S[ss][ch].gather()
-        w[rb(k), wl(k)] = mbuf[...]
-        l[rb(k), rb(k)] = ubuf[...].T
+        w[rb(k), :] = mbuf[...]
+        u[rb(k), rb(k)] = ubuf[...]
         end = max(CHUNKS[ch][1] for ch in range(nc) if JOIN[s][ch] < t)
-        eliminate(k, k + 1, end, g, l, w)
+        eliminate(k, k + 1, end, g, u, w)
         for ch in range(nc):
             if JOIN[s][ch] == t:
                 S[s][ch].finish(g)
                 a, b, _ = CHUNKS[ch]
                 for j in range(k + 1):
-                    eliminate(j, a, b, g, l, w)
+                    eliminate(j, a, b, g, u, w)
         if k < NB - 1:
             dbuf[...] = g[rb(k + 1), rb(k + 1)]
-        if k % 2:
-            pair(k, l, w)
+        invert_pair(k, u, w, wt)
         if t in APPLY:
             ch = APPLY[t]
             a, b, _ = CHUNKS[ch]
-            solve_cols(x, l, w, q, a, b)
+            solve_cols(x, u, wt, q, a, b)
             S1[ch].gram(q)
             S1[ch].swap()
         if t == NB - 1:
@@ -317,7 +327,7 @@
             ch.drain()
 
 
-def last_kernel(x, w, l2, l1, qo, ro, q, r, sem):
+def last_kernel(x, wt, u2, u1, qo, ro, q, r, sem):
     def blk(i):
         return pl.ds(pl.multiple_of(256 * i, 256), 256)
 
@@ -328,24 +338,24 @@
     def diag(d):
         def f(i, _):
             k = pl.ds(pl.multiple_of(256 * i, 256), 256 * (d + 1))
-            r[blk(i), blk(i + d)] = dot(l2[k, blk(i)], l1[blk(i + d), k], ((0,), (1,)))
+            r[blk(i), blk(i + d)] = dot(u2[blk(i), k], u1[k, blk(i + d)], NN)
             return 0
         lax.fori_loop(0, 3 - d, f, 0)
     for d in range(3):
         diag(d)
     out = pltpu.make_async_copy(r, ro, sem.at[0])
     out.start()
-    half = x.shape[0] // 2
+    part = x.shape[0] // 4
 
     def rows(h, _):
-        sl = pl.ds(pl.multiple_of(half * h, half), half)
+        sl = pl.ds(pl.multiple_of(part * h, part), part)
         for j in range(3):
-            solve_rows(x, l2, w, q, 2 * j, 2 * j + 2, sl)
+            solve_rows(x, u2, wt, q, 2 * j, 2 * j + 2, sl)
         pltpu.make_async_copy(q.at[sl], qo.at[sl], sem.at[h + 1]).start()
         return 0
-    lax.fori_loop(0, 2, rows, 0)
-    for h in range(2):
-        sl = pl.ds(half * h, half)
+    lax.fori_loop(0, 4, rows, 0)
+    for h in range(4):
+        sl = pl.ds(part * h, part)
         pltpu.make_async_copy(q.at[sl], qo.at[sl], sem.at[h + 1]).wait()
     out.wait()
 
@@ -362,13 +372,13 @@
         bufs += [B(2 * h, 128), B(h, 128), B(h, 128), B(UT * NCH, 128), B(2 * h, 128), B(UT, 128)]
 
     def local_qr(a):
-        q1, w2, l1, l2 = pl.pallas_call(
-            main_kernel, out_shape=(F(*a.shape), F(N, 256), F(N, N), F(N, N)), in_specs=[V], out_specs=(V,) * 4,
-            scratch_shapes=[B(N, N), B(N, 256), B(128, 128), B(128, 128), B(128, 128)] + bufs + [pltpu.SemaphoreType.DMA((2, len(CHUNKS)))] * 8,
-            compiler_params=pltpu.CompilerParams(vmem_limit_bytes=34 * 2**20, collective_id=0, has_side_effects=True), name="sweeps")(a)
+        q1, wt2, u1, u2 = pl.pallas_call(
+            main_kernel, out_shape=(F(*a.shape), F(N, 256), F(N, N), F(N, N)), in_specs=[pl.BlockSpec(memory_space=pltpu.HBM)], out_specs=(V,) * 4,
+            scratch_shapes=[B(*a.shape), pltpu.SemaphoreType.DMA((3,)), B(N, N), B(N, 256), B(N, 128), B(128, 128), B(128, 128), B(128, 128)] + bufs + [pltpu.SemaphoreType.DMA((2, len(CHUNKS)))] * 8,
+            compiler_params=pltpu.CompilerParams(vmem_limit_bytes=44 * 2**20, collective_id=0, has_side_effects=True), name="sweeps")(a)
         return tuple(pl.pallas_call(
             last_kernel, out_shape=(F(*a.shape), F(N, N)), in_specs=[V] * 4, out_specs=(H, H),
-            scratch_shapes=[B(*a.shape), B(N, N), pltpu.SemaphoreType.DMA((3,))],
-            compiler_params=pltpu.CompilerParams(vmem_limit_bytes=20 * 2**20), name="last")(q1, w2, l2, l1))
+            scratch_shapes=[B(*a.shape), B(N, N), pltpu.SemaphoreType.DMA((5,))],
+            compiler_params=pltpu.CompilerParams(vmem_limit_bytes=20 * 2**20), name="last")(q1, wt2, u2, u1))
 
     return jax.shard_map(local_qr, mesh=mesh, in_specs=(spec,), out_specs=(spec, P("batch", None)), check_vma=False)

time: 130 us -> 129 us (level)
  local copies, waits for them, and re-layouts: 1.88 us -> 0 us
    unnamed x2 -> x0, local copies, waits for them, and re-layouts: 1.88 us -> none
where the time goes in v2:
time: 129 us
  Pallas kernels  128 us (99%)
    pallas_call x1, Pallas kernels, local_qr(): pl.pallas_call(main_kernel, out_shape=(F(*a.shape), F(N, 256), F(N, N), F...  114 us
    pallas_call x1, Pallas kernels, local_qr(): pl.pallas_call(last_kernel, out_shape=(F(*a.shape), F(N, N)), in_specs=[V...  14 us

profile of v2, /device:TPU:1, one launch (start us, length us, event | category | flops | bytes accessed | tf_op | source)
XLA Modules:
  0.0 128.9 jit_solution(6835396373731291535)
XLA Ops:
  0.6 114.1 %sweeps.1 = (f32[1024,768]{1,0:T(8,128)S(1)}, f32[768,256]{1,0:T(8,128)S(1)}, f32[768,768]{1,0:T(8,128)S(1)}, f32[768,768]{1,0:T(8,128)S(1)}) custom-call(f32[1024,768]{1,0:T(8,128)} %xin.1), custom_call_target="tpu_custom_call" | custom-call | tf_op jit(solution)/shard_map/sweeps/pallas_call | solution.py:375
  114.8 14.0 %last.1 = (f32[1024,768]{1,0:T(8,128)}, f32[768,768]{1,0:T(8,128)}) custom-call(f32[1024,768]{1,0:T(8,128)S(1)} %get-tuple-element.6.x, f32[768,256]{1,0:T(8,128)S(1)} %get-tuple-element.7.wt, f32[768,768]{1,0:T(8,128)S(1)} %get-tuple-element.8.u2, f32[768,768]{1,0:T(8,128)S(1)} %get-tuple-element.9.u1), custom_call_target="tpu_custom_call" | custom-call | tf_op jit(solution)/shard_map/last/pallas_call | solution.py:379

commit v3 on v2

--- a/solution.py
+++ b/solution.py
@@ -252,8 +252,9 @@
     bufs, sems = rest[:12 * nc], rest[12 * nc:]
     S = [[Sum(ch, c, me, bufs[6 * (nc * s + ch):6 * (nc * s + ch) + 6], [r.at[s, ch] for r in sems]) for ch in range(nc)] for s in range(2)]
     S0, S1 = S
-    for r in (wt1, wt2, u1, u2):
-        r[...] = jnp.zeros_like(r)
+    for k in range(1, NB, 2):
+        for r, j in ((u1, k - 1), (u2, k - 1), (wt1, 0), (wt2, 0)):
+            r[rb(k), rb(j)] = jnp.zeros((128, 128), jnp.float32)
     for ch in range(2):
         load[ch].wait()
         S0[ch].gram(x)
@@ -267,9 +268,10 @@
         S0[ch].scatter()
     S0[3].gram(x)
     S0[3].swap()
-    for ch in (2, 3):
-        S0[ch].scatter()
-    for ch in range(3):
+    S0[2].scatter()
+    S0[0].reduce()
+    S0[3].scatter()
+    for ch in (1, 2):
         S0[ch].reduce()
     S0[0].gather()
     S0[0].finish(g)

time: 129 us -> 129 us (level)
  no operation moved by 1% of the time
where the time goes in v3:
time: 129 us
  Pallas kernels  128 us (99%)
    pallas_call x1, Pallas kernels, local_qr(): pl.pallas_call(main_kernel, out_shape=(F(*a.shape), F(N, 256), F(N, N), F...  114 us
    pallas_call x1, Pallas kernels, local_qr(): pl.pallas_call(last_kernel, out_shape=(F(*a.shape), F(N, N)), in_specs=[V...  14 us

profile of v3, /device:TPU:1, one launch (start us, length us, event | category | flops | bytes accessed | tf_op | source)
XLA Modules:
  0.0 128.9 jit_solution(2145554555481259169)
XLA Ops:
  0.6 114.1 %sweeps.1 = (f32[1024,768]{1,0:T(8,128)S(1)}, f32[768,256]{1,0:T(8,128)S(1)}, f32[768,768]{1,0:T(8,128)S(1)}, f32[768,768]{1,0:T(8,128)S(1)}) custom-call(f32[1024,768]{1,0:T(8,128)} %xin.1), custom_call_target="tpu_custom_call" | custom-call | tf_op jit(solution)/shard_map/sweeps/pallas_call | solution.py:377
  114.8 14.0 %last.1 = (f32[1024,768]{1,0:T(8,128)}, f32[768,768]{1,0:T(8,128)}) custom-call(f32[1024,768]{1,0:T(8,128)S(1)} %get-tuple-element.6.x, f32[768,256]{1,0:T(8,128)S(1)} %get-tuple-element.7.wt, f32[768,768]{1,0:T(8,128)S(1)} %get-tuple-element.8.u2, f32[768,768]{1,0:T(8,128)S(1)} %get-tuple-element.9.u1), custom_call_target="tpu_custom_call" | custom-call | tf_op jit(solution)/shard_map/last/pallas_call | solution.py:381
